TPU v7x, 512 devices: a whole 4x4x16 slice. The times are simulated.
512 devices in a mesh: dp: 64 (over x, z_lo, core), mp: 8 (over z_hi, y).
Axes of the slice: x: 4, y: 4, z: 16 (z_hi: 2, z_lo: 8; z = z_hi * 8 + z_lo), core: 2. Of those that a mesh axis runs over, the one named last changes fastest.
Arguments:
- tokens: bfloat16 [768, 4608], P('dp', 'mp'), may hold values from -6 to 6
- frozen_weight: bfloat16 [2, 4608, 36864], P(None, 'mp', 'dp'), may hold values from -36 to 36
- adapter_down: bfloat16 [2, 16, 4608], P(None, None, 'mp'), may hold values from -1.5 to 1.5
- adapter_up: bfloat16 [2, 16, 36864], P(None, None, 'dp'), may hold values from -3 to 3
- magnitude: float32 [2, 36864], P(None, 'dp'), may hold values from 0.5 to 2
- hidden_gradient: bfloat16 [768, 36864], P('mp', 'dp'), may hold values from -0.59765625 to 0.59765625
Outputs:
- hidden: bfloat16 [768, 36864], P('mp', 'dp')
- token_gradient: float32 [768, 4608], P('dp', 'mp')
- adapter_down_gradient: float32 [2, 16, 4608], P(None, None, 'mp')
- adapter_up_gradient: float32 [2, 16, 36864], P(None, None, 'dp')
- magnitude_gradient: float32 [2, 36864], P(None, 'dp')
All inputs are finite; a program needn't handle non-finite values.
Results may differ from a plain program's by a relative error of at most 0.023.
Values may be sent and summed in bfloat16 or wider, within the bound.
A program may use at most 64 MiB of HBM per device.

v0:
```python
import jax
import jax.numpy as jnp
from jax import lax
from jax.sharding import PartitionSpec as P

LOWRANK_SCALE = 2.0
EPSILON = 1e-06
MATMUL_ACCURACY = lax.Precision.HIGHEST


def copy_for_each(array, axis):
    copies = jnp.broadcast_to(array, (lax.axis_size(axis), *array.shape))
    return lax.all_to_all(copies, axis, split_axis=0, concat_axis=0, tiled=True)


def taken_together(array, axis):
    everything = copy_for_each(array, axis)
    return jnp.sum(everything.astype(jnp.float32), axis=0)


def over_pieces(array, axis):
    tiles = lax.all_gather(array, axis)
    return tiles.sum(axis=0)


def cut_along(array, dim, size):
    lengths = array.shape
    tiles = array.reshape(*lengths[:dim], size, lengths[dim] // size, *lengths[dim + 1 :])
    return jnp.moveaxis(tiles, dim, 0)


def sum_at_owner(array, axis, dim):
    size = lax.axis_size(axis)
    tiles = lax.all_to_all(cut_along(array, dim, size), axis, 0, 0, tiled=True)
    return jnp.sum(tiles.astype(jnp.float32), axis=0)


def gelu_pair(source):
    cubic_term = source + 0.044715 * source * source * source
    tangent = jnp.tanh(0.7978845608028654 * cubic_term)
    result = 0.5 * source * (1.0 + tangent)
    derivative = 0.5 * (1.0 + tangent) + 0.5 * source * (
        1.0 - tangent * tangent
    ) * 0.7978845608028654 * (1.0 + 0.134145 * source * source)
    return (result, derivative)


def on_device(tokens, frozen_weight, adapter_down, adapter_up, magnitude, hidden_gradient):
    every_row = lax.all_gather(tokens, "dp", axis=0, tiled=True)
    down_broad = adapter_down.astype(jnp.float32)
    up_broad = adapter_up.astype(jnp.float32)
    combined_weight = frozen_weight.astype(jnp.float32) + LOWRANK_SCALE * jnp.einsum(
        "ipq,iph->iqh", adapter_down, adapter_up, preferred_element_type=jnp.float32
    )
    square_part = jnp.sum(combined_weight * combined_weight, axis=1)
    cross_part = jnp.einsum("krd,kdf->krf", down_broad, combined_weight, precision=MATMUL_ACCURACY)
    square_sum, mixed_sum = (
        taken_together(square_part.astype(jnp.bfloat16), "mp").astype(jnp.float32),
        taken_together(cross_part.astype(jnp.bfloat16), "mp").astype(jnp.float32),
    )
    base_part = jnp.einsum(
        "td,kdf->ktf", every_row, frozen_weight, preferred_element_type=jnp.float32
    )
    lowrank_piece = jnp.einsum(
        "su,vgu->vsg", every_row, adapter_down, preferred_element_type=jnp.float32
    )
    col_norm = jnp.sqrt(square_sum + EPSILON)
    col_ratio = magnitude / col_norm
    share_rows = every_row.shape[0] // lax.axis_size("mp")
    base_sum, low_sum = (
        lax.psum(base_part.astype(jnp.bfloat16), "mp").astype(jnp.float32),
        lax.psum(lowrank_piece.astype(jnp.bfloat16), "mp").astype(jnp.float32),
    )
    cot_rows = lax.all_gather(hidden_gradient, "mp", axis=0, tiled=True)
    token_lowrank = low_sum.astype(jnp.bfloat16)
    unscaled_output = base_sum + LOWRANK_SCALE * jnp.einsum(
        "hls,hse->hle", token_lowrank, adapter_up, preferred_element_type=jnp.float32
    )
    gate_proj = unscaled_output[0] * col_ratio[0]
    up_proj = unscaled_output[1] * col_ratio[1]
    activated, derivative = gelu_pair(gate_proj)
    hidden_rows = (activated * up_proj).astype(jnp.bfloat16)
    cotangent = cot_rows.astype(jnp.float32)
    grad_out = jnp.stack([cotangent * up_proj * derivative, cotangent * activated])
    moment_part = jnp.sum(grad_out * unscaled_output, axis=1)
    prescale_gradient = (grad_out * col_ratio[:, None, :]).astype(jnp.bfloat16)
    lowrank_gradient_piece = jnp.einsum(
        "hmu,hmq->huq", token_lowrank, prescale_gradient, preferred_element_type=jnp.float32
    )
    hidden = lax.dynamic_slice_in_dim(hidden_rows, lax.axis_index("mp") * share_rows, share_rows, 0)
    magnitude_gradient = moment_part / col_norm
    frozen_term = -magnitude * moment_part / (col_norm * col_norm * col_norm)
    adapter_up_gradient = LOWRANK_SCALE * (
        lowrank_gradient_piece + mixed_sum * frozen_term[:, None, :]
    )
    lowrank_gradient = jnp.einsum(
        "pge,pbe->pgb", prescale_gradient, adapter_up, preferred_element_type=jnp.float32
    ).astype(jnp.bfloat16)
    weighted_adapter_up = up_broad * frozen_term[:, None, :]
    broadcast_value = jnp.einsum(
        "krf,kdf->krd", weighted_adapter_up, combined_weight, precision=MATMUL_ACCURACY
    )
    down_piece = LOWRANK_SCALE * (
        jnp.einsum("ijp,jv->ipv", lowrank_gradient, every_row, preferred_element_type=jnp.float32)
        + broadcast_value
    )
    adapter_down_gradient = over_pieces(down_piece, "dp")
    main_term = jnp.einsum(
        "ktf,kdf->td", prescale_gradient, frozen_weight, preferred_element_type=jnp.float32
    )
    token_gradient = sum_at_owner(
        (
            main_term
            + LOWRANK_SCALE
            * jnp.einsum(
                "ijf,ifh->jh", lowrank_gradient, adapter_down, preferred_element_type=jnp.float32
            )
        ).astype(jnp.bfloat16),
        "dp",
        0,
    )
    return (hidden, token_gradient, adapter_down_gradient, adapter_up_gradient, magnitude_gradient)


def solution(mesh):
    in_specs = (
        P("dp", "mp"),
        P(None, "mp", "dp"),
        P(None, None, "mp"),
        P(None, None, "dp"),
        P(None, "dp"),
        P("mp", "dp"),
    )
    out_specs = (
        P("mp", "dp"),
        P("dp", "mp"),
        P(None, None, "mp"),
        P(None, None, "dp"),
        P(None, "dp"),
    )
    return jax.shard_map(
        on_device, mesh=mesh, in_specs=in_specs, out_specs=out_specs, check_vma=False
    )
```

profile of v0, /device:TPU:1, one launch (start us, length us, event | category | flops | bytes accessed | tf_op | source)
XLA Modules:
  0.0 562.8 jit_solution(15658596559570055648)
XLA Ops:
  7.2 0.0 copy-start
  7.2 0.0 all-reduce.2.cloned.1.call-start
  7.2 132.6 %all-gather.1 = bf16[64,12,576]{2,1,0:T(8,128)(2,1)S(1)} all-gather(bf16[1,12,576]{2,1,0:T(8,128)(2,1)} %bitcast.68), channel_id=1, replica_groups=mesh['dp'=64,'mp'=8] {'dp'}, dimensions={0}, use_global_device_ids=true | all-gather | bytes 898560 | tf_op jit(solution)/shard_map/all_gather | solution.py:49
  139.9 0.5 reshape.18
  140.4 0.0 copy-start.3
  140.4 4.6 convert_bitcast_fusion
  145.0 0.0 copy-done.3
  145.0 0.0 all-reduce.2.cloned.1.call-update
  145.0 0.0 copy-done
  145.0 0.7 copy-done.6
  145.7 2.1 multiply_reduce_fusion.1
  147.9 0.6 broadcast_in_dim.4
  148.5 10.0 %all-to-all-start = ((bf16[8,2,576]{2,1,0:T(2,128)(2,1)}), bf16[8,2,576]{2,1,0:T(2,128)(2,1)S(1)}, u32[]{:S(2)}, u32[]{:S(2)}) async-start(bf16[8,2,576]{2,1,0:T(2,128)(2,1)} %broadcast_in_dim.4), calls=%async_computation | async-start | bytes 40960 | tf_op jit(solution)/shard_map/all_to_all | solution.py:13
  158.5 0.0 all-gather.4.cloned.1.call-start
  158.6 123.3 %all_gather.13 = bf16[768,576]{1,0:T(8,128)(2,1)} all-gather(bf16[96,576]{1,0:T(8,128)(2,1)S(1)} %copy-done.7), channel_id=1, replica_groups=mesh['dp'=64,'mp'=8] {'mp'}, dimensions={0}, use_global_device_ids=true | all-gather | bytes 995328 | tf_op jit(solution)/shard_map/all_gather | solution.py:74
  281.8 1.6 fusion.14
  283.4 2.3 copy.48
  285.7 84.4 %psum.15 = bf16[2,768,16]{1,2,0:T(8,128)(2,1)S(1)} all-reduce(bf16[2,768,16]{1,2,0:T(8,128)(2,1)S(1)} %fusion.14), channel_id=1, replica_groups=mesh['dp'=64,'mp'=8] {'mp'}, use_global_device_ids=true, to_apply=%region_1.0 | all-reduce | flops 24576 | bytes 98304 | tf_op jit(solution)/shard_map/psum | solution.py:72
  370.1 0.0 all-to-all-done
  370.2 0.0 copy-done.8
  370.2 10.9 %all-reduce.2.cloned.1.call-done = bf16[2,768,576]{1,2,0:T(8,128)(2,1)} async-done(((bf16[2,768,576]{1,2,0:T(8,128)(2,1)}), bf16[2,768,576]{1,2,0:T(8,128)(2,1)}) %all-reduce.2.cloned.1.call-update) | async-done | bytes 1769488 | tf_op jit(solution)/shard_map/psum | solution.py:71
  381.1 2.2 multiply_add_fusion
  383.3 3.1 fusion.2
  386.4 0.6 multiply_reduce_fusion
  387.1 1.2 copy-done.1
  388.3 0.4 convolution_convert_fusion
  388.7 0.2 copy-done.4
  388.9 0.3 fusion.16
  389.2 0.6 fusion.25
  389.8 3.3 fusion.13
  393.1 0.0 all-gather.4.cloned.1.call-update
  393.1 1.1 fusion.15
  394.2 0.8 broadcast_in_dim.10
  395.0 12.7 %all-to-all-start.2 = ((bf16[8,2,16,576]{3,2,1,0:T(8,128)(2,1)}), bf16[8,2,16,576]{3,2,1,0:T(8,128)(2,1)S(1)}, u32[]{:S(2)}, u32[]{:S(2)}) async-start(bf16[8,2,16,576]{3,2,1,0:T(8,128)(2,1)} %broadcast_in_dim.10), calls=%async_computation.2 | async-start | bytes 655360 | tf_op jit(solution)/shard_map/all_to_all | solution.py:13
  407.7 3.3 fusion.28
  411.0 0.4 fusion.11
  411.4 0.6 copy.49
  412.1 1.2 reshape.15
  413.3 9.6 %all-to-all-done.2 = bf16[8,2,16,576]{3,2,1,0:T(8,128)(2,1)S(1)} async-done(((bf16[8,2,16,576]{3,2,1,0:T(8,128)(2,1)}), bf16[8,2,16,576]{3,2,1,0:T(8,128)(2,1)S(1)}, u32[]{:S(2)}, u32[]{:S(2)}) %all-to-all-start.2) | async-done | bytes 294944 | tf_op jit(solution)/shard_map/all_to_all | solution.py:13
  422.9 12.9 %all-to-all-start.1 = ((bf16[64,12,576]{2,1,0:T(8,128)(2,1)}), bf16[64,12,576]{2,1,0:T(8,128)(2,1)S(1)}, u32[]{:S(2)}, u32[]{:S(2)}) async-start(bf16[64,12,576]{2,1,0:T(8,128)(2,1)} %reshape.15), calls=%async_computation.1 | async-start | bytes 2621440 | tf_op jit(solution)/shard_map/all_to_all | solution.py:34
  435.8 0.7 convert_reduce_fusion.1
  436.5 1.5 fusion.20
  438.0 0.8 copy.51
  438.7 2.1 fusion.12
  440.8 69.1 %all-to-all-done.1 = bf16[64,12,576]{2,1,0:T(8,128)(2,1)S(1)} async-done(((bf16[64,12,576]{2,1,0:T(8,128)(2,1)}), bf16[64,12,576]{2,1,0:T(8,128)(2,1)S(1)}, u32[]{:S(2)}, u32[]{:S(2)}) %all-to-all-start.1) | async-done | bytes 884768 | tf_op jit(solution)/shard_map/all_to_all | solution.py:34
  510.0 0.9 convert_reduce_fusion
  510.8 41.7 %all-gather.4.cloned.1.call-done = f32[128,16,576]{2,1,0:T(8,128)} async-done(((f32[2,16,576]{2,1,0:T(8,128)}), f32[128,16,576]{2,1,0:T(8,128)}) %all-gather.4.cloned.1.call-update) | async-done | bytes 4718608 | tf_op jit(solution)/shard_map/all_gather | solution.py:22
  552.6 3.4 reduce_sum.58
  (13 shorter events, 0.1 us)
Async XLA Ops:
  7.2 137.8 %copy-start = (bf16[2,16,576]{2,1,0:T(8,128)(2,1)S(1)}, bf16[2,16,576]{2,1,0:T(8,128)(2,1)}, u32[]{:S(2)}) copy-start(bf16[2,16,576]{2,1,0:T(8,128)(2,1)} %param.8) | copy-start | bytes 110596
  7.2 373.9 %all-reduce.2.cloned.1.call-start = ((), (), s32[]{:S(2)}) async-start(), calls=%async_computation.3 | async-start | bytes 3538944 | tf_op jit(solution)/shard_map/psum | solution.py:71
  140.4 4.6 copy-start.3
  145.0 0.8 copy-start.6
  145.7 12.8 %copy-start.7 = (bf16[96,576]{1,0:T(8,128)(2,1)S(1)}, bf16[96,576]{1,0:T(8,128)(2,1)}, u32[]{:S(2)}) copy-start(bf16[96,576]{1,0:T(8,128)(2,1)} %param.11) | copy-start | bytes 331780
  148.5 221.6 %all-to-all-start = ((bf16[8,2,576]{2,1,0:T(2,128)(2,1)}), bf16[8,2,576]{2,1,0:T(2,128)(2,1)S(1)}, u32[]{:S(2)}, u32[]{:S(2)}) async-start(bf16[8,2,576]{2,1,0:T(2,128)(2,1)} %broadcast_in_dim.4), calls=%async_computation | async-start | bytes 40960 | tf_op jit(solution)/shard_map/all_to_all | solution.py:13
  158.5 394.0 %all-gather.4.cloned.1.call-start = ((), (), s32[]{:S(2)}) async-start(), calls=%async_computation.4 | async-start | bytes 5324800 | tf_op jit(solution)/shard_map/all_gather | solution.py:22
  281.8 88.3 %copy-start.8 = (f32[2,576]{1,0:T(2,128)S(1)}, f32[2,576]{1,0:T(2,128)}, u32[]{:S(2)}) copy-start(f32[2,576]{1,0:T(2,128)} %param.10) | copy-start | bytes 13828
  381.1 2.2 copy-start.5
  387.1 1.3 copy-start.1
  387.1 1.8 copy-start.4
  395.0 27.9 %all-to-all-start.2 = ((bf16[8,2,16,576]{3,2,1,0:T(8,128)(2,1)}), bf16[8,2,16,576]{3,2,1,0:T(8,128)(2,1)S(1)}, u32[]{:S(2)}, u32[]{:S(2)}) async-start(bf16[8,2,16,576]{3,2,1,0:T(8,128)(2,1)} %broadcast_in_dim.10), calls=%async_computation.2 | async-start | bytes 655360 | tf_op jit(solution)/shard_map/all_to_all | solution.py:13
  413.3 25.5 %copy-start.2 = (bf16[2,768,576]{1,2,0:T(8,128)(2,1)S(1)}, bf16[2,768,576]{1,2,0:T(8,128)(2,1)}, u32[]{:S(2)}) copy-start(bf16[2,768,576]{1,2,0:T(8,128)(2,1)} %copy-done.1) | copy-start | bytes 5308420
  422.9 87.1 %all-to-all-start.1 = ((bf16[64,12,576]{2,1,0:T(8,128)(2,1)}), bf16[64,12,576]{2,1,0:T(8,128)(2,1)S(1)}, u32[]{:S(2)}, u32[]{:S(2)}) async-start(bf16[64,12,576]{2,1,0:T(8,128)(2,1)} %reshape.15), calls=%async_computation.1 | async-start | bytes 2621440 | tf_op jit(solution)/shard_map/all_to_all | solution.py:34
Sparse Core Ops, SparseCore 0:
  145.1 235.9 all-reduce.1
  393.2 159.2 all-gather.3
where the time goes:
time: 564 us; the launch traced here: 563 us
  blocking collectives  340 us (60%)
  waiting for transfers between devices  131 us (23%)
  starting transfers between devices  35.7 us (6%)
  matrix products  21.3 us (4%)
  between operations  14.2 us (3%)
  other arithmetic  10.9 us (2%)
  local copies, waits for them, and re-layouts  9.06 us (2%)
    all_gather x1, blocking collectives, on_device(): every_row = lax.all_gather(tokens, 'dp', axis=0, tiled=True)  133 us
    all_gather x1, blocking collectives, on_device(): cot_rows = lax.all_gather(hidden_gradient, 'mp', axis=0, tiled=True)  123 us
    psum x1, blocking collectives, on_device(): lax.psum(lowrank_piece.astype(jnp.bfloat16), 'mp').astype(jnp.float32)  84.4 us
    all_to_all x1, waiting for transfers between devices, sum_at_owner(): tiles = lax.all_to_all(cut_along(array, dim, size), axis, 0, 0, tiled=True)  69.1 us
    all_gather x1, waiting for transfers between devices, over_pieces(): tiles = lax.all_gather(array, axis)  41.7 us
    all_to_all x2, starting transfers between devices, copy_for_each(): return lax.all_to_all(copies, axis, split_axis=0, concat_axis=0, tiled=True)  22.7 us
    all_to_all x1, starting transfers between devices, sum_at_owner(): tiles = lax.all_to_all(cut_along(array, dim, size), axis, 0, 0, tiled=True)  12.9 us
  transfers between devices with their start and end apart: 5, of which 4 were waited for; matrix products, arithmetic and copies ran while one was open for 4% of the time, Pallas kernels for 0%

commit v1 on v0

v1 whole, which is shorter than its diff:
```python
import functools

import jax
import jax.numpy as jnp
from jax import lax
from jax.experimental import pallas as pl
from jax.experimental.pallas import tpu as pltpu
from jax.sharding import PartitionSpec as P

SCALE = 2.0
EPSILON = 1e-06
MESH = pl.DeviceIdType.MESH
F32 = jnp.float32
BF16 = jnp.bfloat16
NT = (((1,), (1,)), ((), ()))
TN = (((0,), (0,)), ((), ()))
NN = (((1,), (0,)), ((), ()))

NX, NY, NZ, NH, NC = 4, 4, 8, 2, 2
ROWS = 96
MINI = 12
WIDE = 576
RANK = 16
STEP = 32
PARTS = ROWS // STEP
CHUNKS = PARTS * NH
BLOCK = NY * STEP


def dot(a, b, dims=NN):
    return lax.dot_general(a, b, dims, preferred_element_type=F32)


def wide_dot(a, b, dims=NN):
    total = None
    for _ in range(3):
        term = a.astype(BF16)
        a = a - term.astype(F32)
        value = dot(term, b, dims)
        total = value if total is None else total + value
    return total


def gelu_pair(source):
    square = source * source
    tangent = jnp.tanh(0.7978845608028654 * (source + 0.044715 * source * square))
    half = 0.5 * (1.0 + tangent)
    slope = half + 0.5 * source * (1.0 - tangent * tangent) * 0.7978845608028654 * (
        1.0 + 0.134145 * square
    )
    return source * half, slope


def kernel(
    tok, w, down, up, mag, cot,
    hid, tg, dg, ug, mg,
    zin, zflat, xb, sq, low_t, up_wide, part, ypart, zpart_out, zpart_in, cots, grad,
    mom, mom_all, acc_d, acc_u, cross, tb, tpair, tsum, tx, tflat, zout, zback,
    d_pair_out, d_pair_in, d_x, d_z, d_last, u_y, u_z,
    zs, zr, xs, xr, cs, cr, qs, qr, ts, tr, ps, pr, ss, sr, gs, gr, ms, mr,
    fs, fr, fxs, fxr, bs, br, ds1, dr1, ds2, dr2, ds3, dr3, ds4, dr4, us1, ur1, us2, ur2,
):
    dp = lax.axis_index("dp")
    mp = lax.axis_index("mp")
    c = lax.rem(dp, NC)
    zl = lax.rem(dp // NC, NZ)
    x = dp // (NC * NZ)
    y = lax.rem(mp, NY)
    zh = mp // NY
    half = zl // 4
    slot = lax.rem(zl, 4) * 2 + c
    mine = half == c

    def at(x=x, zl=zl, c=c, zh=zh, y=y):
        return ((x * NZ + zl) * NC + c, zh * NY + y)

    def send(src, dst, s, r, device):
        return pltpu.make_async_remote_copy(
            src_ref=src, dst_ref=dst, send_sem=s, recv_sem=r,
            device_id=device, device_id_type=MESH,
        )

    partner = at(c=1 - c)
    across = at(zh=1 - zh)
    xnext = [lax.rem(x + d, NX) for d in range(1, NX)]
    ynext = [lax.rem(y + d, NY) for d in range(1, NY)]
    xdev = [at(x=v) for v in xnext]
    ydev = [at(y=v) for v in ynext]

    barrier = pltpu.get_barrier_semaphore()
    greeted = 0
    for k in range(1, NZ):
        for other in (c, 1 - c):
            pl.semaphore_signal(
                barrier, 1, device_id=at(zl=lax.rem(zl + k, NZ), c=other), device_id_type=MESH
            )
            greeted += 1
    for device in [partner, across] + xdev + ydev + [at(zh=1 - zh, y=v) for v in ynext]:
        pl.semaphore_signal(barrier, 1, device_id=device, device_id_type=MESH)
        greeted += 1

    for k in range(2):
        merged = w[k].astype(F32) + SCALE * dot(down[k], up[k], TN)
        sq[mp, pl.ds(k, 1), :] = jnp.sum(merged * merged, axis=0, keepdims=True)

    pl.semaphore_wait(barrier, greeted)

    zcopies = []
    for t in range(NZ):
        zcopies.append(send(tok, zin.at[slot], zs.at[t], zr.at[slot], at(zl=t, c=half)))

        @pl.when(jnp.logical_not(jnp.logical_and(mine, zl == t)))
        def _():
            zcopies[t].start()

    @pl.when(mine)
    def _():
        zin[slot] = tok[...]

    qcopies = []
    for i, device in enumerate(ydev + [across] + [at(zh=1 - zh, y=v) for v in ynext]):
        qcopies.append(send(sq.at[mp], sq.at[mp], qs.at[i], qr.at[mp], device))
        qcopies[-1].start()

    cots[zh] = cot[...]
    for k in range(2):
        up_wide[k] = jnp.zeros((2 * RANK, WIDE), BF16)
        up_wide[k, RANK * k : RANK * (k + 1), :] = (SCALE * up[k].astype(F32)).astype(BF16)
        gram = dot(down[k], down[k], NT)
        cross[k] = dot(down[k], w[k]) + SCALE * wide_dot(gram, up[k])
    mom[...] = jnp.zeros_like(mom)
    acc_d[...] = jnp.zeros_like(acc_d)
    acc_u[...] = jnp.zeros_like(acc_u)
    down_both = down[...].reshape(2 * RANK, WIDE)

    for s in range(8):

        @pl.when(jnp.logical_not(jnp.logical_and(mine, slot == s)))
        def _():
            send(tok, zin.at[s], zs.at[0], zr.at[s], partner).wait_recv()

        zflat[MINI * s : MINI * (s + 1), :] = zin[s].astype(F32)
    own = x * 2 + c
    xb[own] = zflat[...].astype(BF16)

    xcopies = []
    for d in range(3):
        xcopies.append(send(xb.at[own], xb.at[own], xs.at[d], xr.at[x], xdev[d]))
        xcopies[-1].start()
    ccopies = [send(xb.at[own], xb.at[own], cs.at[x], cr.at[x], partner)]
    ccopies[-1].start()
    tcopy = send(cot, cots.at[zh], ts, tr, across)
    tcopy.start()
    for v in [lax.rem(x + 3, NX), xnext[0], xnext[1]]:
        block = xb.at[v * 2 + c]
        send(block, block, xs.at[0], xr.at[v], partner).wait_recv()
        ccopies.append(send(block, block, cs.at[v], cr.at[v], partner))
        ccopies[-1].start()
    for v in range(NX):
        block = xb.at[v * 2 + 1 - c]
        send(block, block, cs.at[0], cr.at[v], partner).wait_recv()

    def place(q):
        return q // NH, lax.rem(q, NH) if not isinstance(q, int) else q % NH

    def rows_of(q):
        r, h = place(q)
        return xb[NY * h : NY * (h + 1), STEP * r : STEP * (r + 1), :].reshape(BLOCK, WIDE)

    pcopies = []

    def products(q):
        lhs = rows_of(q)
        low = dot(lhs, down_both, NT).astype(BF16)
        low_t[q] = dot(down_both, lhs, NT).astype(BF16)
        for k in range(2):
            value = dot(lhs, w[k]) + dot(low, up_wide[k])
            part[q, :, k] = value.astype(BF16).reshape(NY, STEP, WIDE)
        for d in range(3):
            pcopies.append(
                send(part.at[q, ynext[d]], ypart.at[q, d], ps.at[q, d], pr.at[q, d], ydev[d])
            )
            pcopies[-1].start()

    scopies = []

    def over_y(q):
        total = part[q, y].astype(F32)
        for d in range(3):
            send(part.at[q, y], ypart.at[q, d], ps.at[q, d], pr.at[q, d], partner).wait_recv()
            total = total + ypart[q, d].astype(F32)
        zpart_out[q] = total.astype(BF16)
        scopies.append(send(zpart_out.at[q], zpart_in.at[q], ss.at[q], sr.at[q], across))
        scopies[-1].start()

    products(0)
    products(1)
    for q in range(CHUNKS):
        over_y(q)
        if q + 2 < CHUNKS:
            products(q + 2)

    for device in range(NH * NY):

        @pl.when(device != mp)
        def _():
            send(sq.at[device], sq.at[device], qs.at[0], qr.at[device], partner).wait_recv()

    norm_square = sq[0]
    for device in range(1, NH * NY):
        norm_square = norm_square + sq[device]
    norm = jnp.sqrt(norm_square + EPSILON)
    ratio = mag[...] / norm
    tcopy.wait_recv()

    gcopies = []

    def activate(q):
        r, h = place(q)
        rows = slice(STEP * r, STEP * (r + 1))
        send(zpart_out.at[q], zpart_in.at[q], ss.at[q], sr.at[q], partner).wait_recv()
        pre = [zpart_out[q, k].astype(F32) + zpart_in[q, k].astype(F32) for k in range(2)]
        gate = pre[0] * ratio[0:1]
        lift = pre[1] * ratio[1:2]
        active, slope = gelu_pair(gate)

        @pl.when(zh == h)
        def _():
            hid[rows, :] = (active * lift).astype(BF16)

        g = cots[h, rows, :].astype(F32)
        outs = [g * lift * slope, g * active]
        for k in range(2):
            mom[k : k + 1, :] += jnp.sum(outs[k] * pre[k], axis=0, keepdims=True)
            grad[q, y, k] = (outs[k] * ratio[k : k + 1]).astype(BF16)
        for d in range(3):
            gcopies.append(
                send(grad.at[q, y], grad.at[q, y], gs.at[q, d], gr.at[q, y], ydev[d])
            )
            gcopies[-1].start()

    fcopies = []

    def backward(q):
        for d in range(3):
            block = grad.at[q, ynext[d]]
            send(block, block, gs.at[q, d], gr.at[q, ynext[d]], partner).wait_recv()
        lhs = rows_of(q)
        total = None
        for k in range(2):
            g = grad[q, :, k].reshape(BLOCK, WIDE)
            low = dot(g, up[k], NT).astype(BF16)
            low_rows = dot(up[k], g, NT).astype(BF16)
            value = dot(g, w[k], NT) + SCALE * dot(low, down[k])
            total = value if total is None else total + value
            acc_d[k] += dot(low_rows, lhs)
            acc_u[k] += dot(low_t[q, RANK * k : RANK * (k + 1), :], g)
        tb[q] = total.astype(BF16).reshape(2, 2, STEP, WIDE)
        for j in range(2):
            fcopies.append(
                send(tb.at[q, j, 1 - c], tpair.at[q, j], fs.at[q, j], fr.at[q, j], partner)
            )
            fcopies[-1].start()

    fxcopies = []

    def over_cores(q):
        r, h = place(q)
        for j in range(2):
            send(tb.at[q, j, c], tpair.at[q, j], fs.at[q, j], fr.at[q, j], partner).wait_recv()
            tsum[q, j] = (tb[q, j, c].astype(F32) + tpair[q, j].astype(F32)).astype(BF16)
            target = NH * h + j
            copy = send(
                tsum.at[q, j], tx.at[r, x], fxs.at[q, j], fxr.at[r, x], at(x=target)
            )
            fxcopies.append((target, copy))

            @pl.when(x != target)
            def _():
                copy.start()

    for q in range(CHUNKS):
        activate(q)
        if q == CHUNKS - 1:
            mom_all[y] = mom[...]
            mcopies = []
            for d in range(3):
                mcopies.append(send(mom_all.at[y], mom_all.at[y], ms.at[d], mr.at[y], ydev[d]))
                mcopies[-1].start()
        if q:
            over_cores(q - 1)
        backward(q)

    for v in ynext:
        send(mom_all.at[v], mom_all.at[v], ms.at[0], mr.at[v], partner).wait_recv()
    moment = mom_all[0]
    for v in range(1, NY):
        moment = moment + mom_all[v]
    mg[...] = moment / norm
    term = -mag[...] * moment / (norm * norm * norm)
    for k in range(2):
        u_y[y, RANK * k : RANK * (k + 1), :] = (
            SCALE * (acc_u[k] + cross[k] * term[k : k + 1])
        ).astype(BF16)
    u1 = []
    for d in range(3):
        u1.append(send(u_y.at[y], u_y.at[y], us1.at[d], ur1.at[y], ydev[d]))
        u1[-1].start()
    for k in range(2):
        weighted = up[k].astype(F32) * term[k : k + 1]
        spread = wide_dot(weighted, w[k], NT)
        spread = spread + SCALE * wide_dot(wide_dot(weighted, up[k], NT), down[k])
        acc_d[k] = SCALE * (acc_d[k] + spread)
    d_pair_out[...] = acc_d[1 - c].astype(BF16)
    d1 = send(d_pair_out, d_pair_in, ds1, dr1, partner)
    d1.start()
    over_cores(CHUNKS - 1)

    d1.wait_recv()
    d_x[x] = (acc_d[c] + d_pair_in[...].astype(F32)).astype(BF16)
    d2 = []
    for d in range(3):
        d2.append(send(d_x.at[x], d_x.at[x], ds2.at[d], dr2.at[x], xdev[d]))
        d2[-1].start()

    for v in ynext:
        send(u_y.at[v], u_y.at[v], us1.at[0], ur1.at[v], partner).wait_recv()
    total_u = u_y[0].astype(F32)
    for v in range(1, NY):
        total_u = total_u + u_y[v].astype(F32)
    u_z[zh] = total_u.astype(BF16)
    u2 = send(u_z.at[zh], u_z.at[zh], us2, ur2.at[zh], across)
    u2.start()

    for r in range(PARTS):
        total = tsum[NH * r + x // 2, lax.rem(x, 2)].astype(F32)
        for v in xnext:
            send(tx.at[r, v], tx.at[r, v], fxs.at[0, 0], fxr.at[r, v], partner).wait_recv()
            total = total + tx[r, v].astype(F32)
        tflat[STEP * r : STEP * (r + 1), :] = total
    bcopies = []
    for s in range(8):
        zout[s] = tflat[MINI * s : MINI * (s + 1), :].astype(BF16)
        copy = send(
            zout.at[s], zback.at[zl], bs.at[s], br.at[zl], at(zl=4 * c + s // 2, c=s % 2)
        )
        bcopies.append(copy)

        @pl.when(jnp.logical_not(jnp.logical_and(mine, slot == s)))
        def _():
            copy.start()

    @pl.when(mine)
    def _():
        zback[zl] = zout[slot]

    for v in xnext:
        send(d_x.at[v], d_x.at[v], ds2.at[0], dr2.at[v], partner).wait_recv()
    total_d = d_x[0].astype(F32)
    for v in range(1, NX):
        total_d = total_d + d_x[v].astype(F32)
    d_z[zl] = total_d.astype(BF16)
    d3 = []
    for k in range(1, NZ):
        d3.append(
            send(d_z.at[zl], d_z.at[zl], ds3.at[k - 1], dr3.at[zl], at(zl=lax.rem(zl + k, NZ)))
        )
        d3[-1].start()

    for t in range(NZ):

        @pl.when(jnp.logical_not(jnp.logical_and(mine, zl == t)))
        def _():
            send(zback.at[t], zback.at[t], bs.at[0], br.at[t], partner).wait_recv()

    total = zback[0].astype(F32)
    for t in range(1, NZ):
        total = total + zback[t].astype(F32)
    tg[...] = total

    for k in range(1, NZ):
        v = lax.rem(zl + k, NZ)
        send(d_z.at[v], d_z.at[v], ds3.at[0], dr3.at[v], partner).wait_recv()
    total_d = d_z[0].astype(F32)
    for t in range(1, NZ):
        total_d = total_d + d_z[t].astype(F32)
    d_last[c] = total_d
    d4 = send(d_last.at[c], d_last.at[c], ds4, dr4.at[c], partner)
    d4.start()

    send(u_z.at[1 - zh], u_z.at[1 - zh], us2, ur2.at[1 - zh], partner).wait_recv()
    ug[...] = (u_z[0].astype(F32) + u_z[1].astype(F32)).reshape(2, RANK, WIDE)
    send(d_last.at[1 - c], d_last.at[1 - c], ds4, dr4.at[1 - c], partner).wait_recv()
    dg[...] = d_last[...]

    for t in range(NZ):

        @pl.when(jnp.logical_not(jnp.logical_and(mine, zl == t)))
        def _():
            zcopies[t].wait_send()

    for s in range(8):

        @pl.when(jnp.logical_not(jnp.logical_and(mine, slot == s)))
        def _():
            bcopies[s].wait_send()

    for target, copy in fxcopies:

        @pl.when(x != target)
        def _():
            copy.wait_send()

    for copy in (
        qcopies + xcopies + ccopies + [tcopy] + pcopies + scopies + gcopies + mcopies
        + fcopies + u1 + [d1] + d2 + [u2] + d3 + [d4]
    ):
        copy.wait_send()


def on_device(tokens, frozen_weight, adapter_down, adapter_up, magnitude, hidden_gradient):
    vmem = pl.BlockSpec(memory_space=pltpu.VMEM)
    dma = pltpu.SemaphoreType.DMA
    scratch = [
        pltpu.VMEM((8, MINI, WIDE), BF16),
        pltpu.VMEM((ROWS, WIDE), F32),
        pltpu.VMEM((8, ROWS, WIDE), BF16),
        pltpu.VMEM((8, 2, WIDE), F32),
        pltpu.VMEM((CHUNKS, 2 * RANK, BLOCK), BF16),
        pltpu.VMEM((2, 2 * RANK, WIDE), BF16),
        pltpu.VMEM((CHUNKS, NY, 2, STEP, WIDE), BF16),
        pltpu.VMEM((CHUNKS, 3, 2, STEP, WIDE), BF16),
        pltpu.VMEM((CHUNKS, 2, STEP, WIDE), BF16),
        pltpu.VMEM((CHUNKS, 2, STEP, WIDE), BF16),
        pltpu.VMEM((NH, ROWS, WIDE), BF16),
        pltpu.VMEM((CHUNKS, NY, 2, STEP, WIDE), BF16),
        pltpu.VMEM((2, WIDE), F32),
        pltpu.VMEM((NY, 2, WIDE), F32),
        pltpu.VMEM((2, RANK, WIDE), F32),
        pltpu.VMEM((2, RANK, WIDE), F32),
        pltpu.VMEM((2, RANK, WIDE), F32),
        pltpu.VMEM((CHUNKS, 2, 2, STEP, WIDE), BF16),
        pltpu.VMEM((CHUNKS, 2, STEP, WIDE), BF16),
        pltpu.VMEM((CHUNKS, 2, STEP, WIDE), BF16),
        pltpu.VMEM((PARTS, NX, STEP, WIDE), BF16),
        pltpu.VMEM((ROWS, WIDE), F32),
        pltpu.VMEM((8, MINI, WIDE), BF16),
        pltpu.VMEM((NZ, MINI, WIDE), BF16),
        pltpu.VMEM((RANK, WIDE), BF16),
        pltpu.VMEM((RANK, WIDE), BF16),
        pltpu.VMEM((NX, RANK, WIDE), BF16),
        pltpu.VMEM((NZ, RANK, WIDE), BF16),
        pltpu.VMEM((2, RANK, WIDE), F32),
        pltpu.VMEM((NY, 2 * RANK, WIDE), BF16),
        pltpu.VMEM((NH, 2 * RANK, WIDE), BF16),
        dma((NZ,)), dma((8,)),
        dma((3,)), dma((NX,)),
        dma((NX,)), dma((NX,)),
        dma((7,)), dma((8,)),
        dma, dma,
        dma((CHUNKS, 3)), dma((CHUNKS, 3)),
        dma((CHUNKS,)), dma((CHUNKS,)),
        dma((CHUNKS, 3)), dma((CHUNKS, NY)),
        dma((3,)), dma((NY,)),
        dma((CHUNKS, 2)), dma((CHUNKS, 2)),
        dma((CHUNKS, 2)), dma((PARTS, NX)),
        dma((8,)), dma((NZ,)),
        dma, dma,
        dma((3,)), dma((NX,)),
        dma((NZ - 1,)), dma((NZ,)),
        dma, dma((2,)),
        dma((3,)), dma((NY,)),
        dma, dma((NH,)),
    ]
    return pl.pallas_call(
        kernel,
        name="dora_step",
        out_shape=(
            jax.ShapeDtypeStruct((ROWS, WIDE), BF16),
            jax.ShapeDtypeStruct((MINI, WIDE), F32),
            jax.ShapeDtypeStruct((2, RANK, WIDE), F32),
            jax.ShapeDtypeStruct((2, RANK, WIDE), F32),
            jax.ShapeDtypeStruct((2, WIDE), F32),
        ),
        in_specs=[vmem] * 6,
        out_specs=(vmem,) * 5,
        scratch_shapes=scratch,
        compiler_params=pltpu.CompilerParams(
            collective_id=0, has_side_effects=True, vmem_limit_bytes=60 * 1024 * 1024
        ),
    )(tokens, frozen_weight, adapter_down, adapter_up, magnitude, hidden_gradient)


def solution(mesh):
    in_specs = (
        P("dp", "mp"),
        P(None, "mp", "dp"),
        P(None, None, "mp"),
        P(None, None, "dp"),
        P(None, "dp"),
        P("mp", "dp"),
    )
    out_specs = (
        P("mp", "dp"),
        P("dp", "mp"),
        P(None, None, "mp"),
        P(None, None, "dp"),
        P(None, "dp"),
    )
    return jax.shard_map(
        on_device, mesh=mesh, in_specs=in_specs, out_specs=out_specs, check_vma=False
    )
```

time: 564 us -> 147 us (0.26)
  blocking collectives: 340 us -> 0 us
  Pallas kernels: 0 us -> 136 us
  waiting for transfers between devices: 131 us -> 0 us
  starting transfers between devices: 35.7 us -> 0 us
  matrix products: 21.3 us -> 0 us
  between operations: 14.2 us -> 0.64 us
  other arithmetic: 10.9 us -> 0 us
    all_gather x2 -> x0, blocking collectives: 256 us -> none  [the longest x1 133 us: on_device(): every_row = lax.all_gather(tokens, 'dp', axis=0, tiled=True)]
    pallas_call x0 -> x1, Pallas kernels: none -> 136 us  [on_device(): pl.pallas_call(kernel, name='dora_step', out_shape=(jax.ShapeDtypeStruct(...]
    psum x1 -> x0, blocking collectives: 84.4 us -> none  [on_device(): lax.psum(lowrank_piece.astype(jnp.bfloat16), 'mp').astype(jnp.float32)]
    all_to_all x3 -> x0, waiting for transfers between devices: 78.7 us -> none  [the longest x1 69.1 us: sum_at_owner(): tiles = lax.all_to_all(cut_along(array, dim, size), axis, 0, 0, tiled=True)]
    all_gather x1 -> x0, waiting for transfers between devices: 41.7 us -> none  [over_pieces(): tiles = lax.all_gather(array, axis)]
    all_to_all x3 -> x0, starting transfers between devices: 35.6 us -> none  [the longest x2 22.7 us: copy_for_each(): return lax.all_to_all(copies, axis, split_axis=0, concat_axis=0, tiled=True)]
    dot_general x11 -> x0, matrix products: 21.3 us -> none  [the longest x1 4.59 us: on_device(): jnp.einsum('td,kdf->ktf', every_row, frozen_weight, preferred_element_typ...]
    psum x1 -> x0, waiting for transfers between devices: 10.9 us -> none  [on_device(): lax.psum(base_part.astype(jnp.bfloat16), 'mp').astype(jnp.float32)]
  transfers between devices with their start and end apart: 5 -> 0, of which waited for: 4 -> 0; matrix products, arithmetic and copies ran while one was open for 4% -> 0% of each run, Pallas kernels for 0% -> 0%
where the time goes in v1:
time: 147 us; the launch traced here: 144 us
  Pallas kernels  136 us (93%)
  local copies, waits for them, and re-layouts  7.29 us (5%)
    pallas_call x1, Pallas kernels, on_device(): pl.pallas_call(kernel, name='dora_step', out_shape=(jax.ShapeDtypeStruct(...  136 us
    unnamed x5, local copies, waits for them, and re-layouts  7.29 us

profile of v1, /device:TPU:1, one launch (start us, length us, event | category | flops | bytes accessed | tf_op | source)
XLA Modules:
  0.0 144.2 jit_solution(4934795837954179933)
XLA Ops:
  0.6 136.2 %dora_step.1 = (bf16[96,576]{1,0:T(8,128)(2,1)}, f32[12,576]{1,0:T(8,128)}, f32[2,16,576]{2,1,0:T(8,128)}, f32[2,16,576]{2,1,0:T(8,128)}, f32[2,576]{1,0:T(2,128)}) custom-call(bf16[12,576]{1,0:T(8,128)(2,1)} %tok.1, bf16[2,576,576]{2,1,0:T(8,128)(2,1)} %w.1, bf16[2,16,576]{2,1,0:T(8,128)(2,1)} %down.1, bf16[2,16,576]{2,1,0:T(8,128)(2,1)} %up.1, ...), custom_call_target="tpu_custom_call" | custom-call | tf_op jit(solution)/shard_map/dora_step/pallas_call | solution.py:475
  136.9 1.6 %copy.16 = bf16[96,576]{1,0:T(8,128)(2,1)} copy(bf16[96,576]{1,0:T(8,128)(2,1)} %get-tuple-element.10) | data formatting | bytes 221184
  138.4 1.4 copy.17
  139.8 1.5 %copy.18 = f32[2,16,576]{2,1,0:T(8,128)} copy(f32[2,16,576]{2,1,0:T(8,128)} %get-tuple-element.12) | data formatting | bytes 147456
  141.4 1.5 %copy.19 = f32[2,16,576]{2,1,0:T(8,128)} copy(f32[2,16,576]{2,1,0:T(8,128)} %get-tuple-element.13) | data formatting | bytes 147456
  142.9 1.3 copy.20

commit v2 on v1

v2 whole, which is shorter than its diff:
```python
import jax
import jax.numpy as jnp
from jax import lax
from jax.experimental import pallas as pl
from jax.experimental.pallas import tpu as pltpu
from jax.sharding import PartitionSpec as P

SCALE = 2.0
EPSILON = 1e-06
MESH = pl.DeviceIdType.MESH
F32 = jnp.float32
BF16 = jnp.bfloat16
NT = (((1,), (1,)), ((), ()))
TN = (((0,), (0,)), ((), ()))
NN = (((1,), (0,)), ((), ()))

NX, NY, NZ, NH, NC = 4, 4, 8, 2, 2
ROWS = 96
MINI = 12
WIDE = 576
RANK = 16
PIECES = ((0, 16), (16, 32), (48, 32), (80, 16))
LEAVES = ((0,), (1, 2, 3), (4, 5), (6, 7))
CHUNKS = len(PIECES) * NH
GROUPS = ((0, 16), (16, 80))
HALVES = ((0, 48), (48, 48))
ORDER = (
    "P0 P1 G P2 S0 P3 S1 P4 S2 P5 S3 H P6 S4 P7 S5 N C0 C1 S6 S7 B0 C2 B1 U0 C3 B2 U1 C4 B3 U2 V0 "
    "C5 B4 U3 C6 B5 U4 V1 C7 M B6 U5 W U6 B7 V2"
).split()


def dot(a, b, dims=NN):
    return lax.dot_general(a, b, dims, preferred_element_type=F32)


def wide_dot(a, b, dims=NN):
    total = None
    for _ in range(3):
        term = a.astype(BF16)
        a = a - term.astype(F32)
        value = dot(term, b, dims)
        total = value if total is None else total + value
    return total


def gelu_pair(source):
    square = source * source
    tangent = jnp.tanh(0.7978845608028654 * (source + 0.044715 * source * square))
    half = 0.5 * (1.0 + tangent)
    slope = half + 0.5 * source * (1.0 - tangent * tangent) * 0.7978845608028654 * (
        1.0 + 0.134145 * square
    )
    return source * half, slope


def kernel(
    tok_in, w_in, down_in, up_in, mag_in, cot_in,
    hid, tg, dg, ug, mg,
    tok, w, down, up, mag,
    zin, zflat, xb, sq, low_t, up_wide, part, ypart, zpart_out, zpart_in, cots, grad,
    mom, mom_all, acc_d, acc_u, cross, tb, tpair, tsum, tx, tflat, zout, zback,
    d_pair_out, d_pair_in, d_x_out, d_x, d_z, d_all, u_out, u_y, u_z, u_all,
    ls, zs, zr, xs, xr, cs, cr, qs, qr, ts, tr, answer, ps, pr, ss, sr, gs, gr, ms, mr,
    fs, fr, fxs, fxr, bs, br, ds1, dr1, ds2, dr2, ds3, dr3, ds4, dr4, us1, ur1, us2, ur2, us3, ur3,
):
    dp = lax.axis_index("dp")
    mp = lax.axis_index("mp")
    c = lax.rem(dp, NC)
    zl = lax.rem(dp // NC, NZ)
    x = dp // (NC * NZ)
    y = lax.rem(mp, NY)
    zh = mp // NY
    half = zl // 4
    slot = lax.rem(zl, 4) * 2 + c
    mine = half == c

    def at(x=x, zl=zl, c=c, zh=zh, y=y):
        return ((x * NZ + zl) * NC + c, zh * NY + y)

    def send(src, dst, s, r, device):
        return pltpu.make_async_remote_copy(
            src_ref=src, dst_ref=dst, send_sem=s, recv_sem=r,
            device_id=device, device_id_type=MESH,
        )

    partner = at(c=1 - c)
    across = at(zh=1 - zh)
    xnext = [lax.rem(x + d, NX) for d in range(1, NX)]
    ynext = [lax.rem(y + d, NY) for d in range(1, NY)]
    xdev = [at(x=v) for v in xnext]
    ydev = [at(y=v) for v in ynext]
    sent = []

    def go(src, dst, s, r, device):
        copy = send(src, dst, s, r, device)
        copy.start()
        sent.append(copy)

    def come(ref, s, r):
        send(ref, ref, s, r, partner).wait_recv()

    barrier = pltpu.get_barrier_semaphore()
    greeted = 0
    for k in range(1, NZ):
        for other in (c, 1 - c):
            pl.semaphore_signal(
                barrier, 1, device_id=at(zl=lax.rem(zl + k, NZ), c=other), device_id_type=MESH
            )
            greeted += 1
    far = [across] + [at(zh=1 - zh, y=v) for v in ynext]
    xpair = [at(x=v, c=1 - c) for v in xnext]
    for device in [partner] + xdev + ydev + xpair:
        pl.semaphore_signal(barrier, 1, device_id=device, device_id_type=MESH)
        greeted += 1

    @pl.when(zh == 0)
    def _():
        for device in far:
            pl.semaphore_signal(barrier, 1, device_id=device, device_id_type=MESH)

    local = [
        pltpu.make_async_copy(a, b, ls.at[i])
        for i, (a, b) in enumerate(
            ((down_in, down), (up_in, up), (w_in, w), (tok_in, tok), (mag_in, mag),
             (cot_in, cots.at[zh]))
        )
    ]
    for copy in local:
        copy.start()

    for copy in local:
        copy.wait()
    for k in range(2):
        merged = w[k].astype(F32) + SCALE * dot(down[k], up[k], TN)
        sq[mp, pl.ds(k, 1), :] = jnp.sum(merged * merged, axis=0, keepdims=True)

    @pl.when(zh == 0)
    def _():
        pl.semaphore_wait(barrier, greeted)

    @pl.when(zh == 1)
    def _():
        pl.semaphore_wait(barrier, greeted + len(far))
        for device in far:
            pl.semaphore_signal(answer, 1, device_id=device, device_id_type=MESH)

    zcopies = []
    for t in range(NZ):
        zcopies.append(send(tok, zin.at[slot], zs.at[t], zr.at[slot], at(zl=t, c=half)))

        @pl.when(jnp.logical_not(jnp.logical_and(mine, zl == t)))
        def _():
            zcopies[t].start()

    @pl.when(mine)
    def _():
        zin[slot] = tok[...]

    for i, device in enumerate(ydev):
        go(sq.at[mp], sq.at[mp], qs.at[i], qr.at[mp], device)

    for k in range(2):
        up_wide[k] = jnp.zeros((2 * RANK, WIDE), BF16)
        up_wide[k, RANK * k : RANK * (k + 1), :] = (SCALE * up[k].astype(F32)).astype(BF16)
        gram = dot(down[k], down[k], NT)
        cross[k] = dot(down[k], w[k]) + SCALE * wide_dot(gram, up[k])
    mom[...] = jnp.zeros_like(mom)
    acc_d[...] = jnp.zeros_like(acc_d)
    acc_u[...] = jnp.zeros_like(acc_u)
    down_both = down[...].reshape(2 * RANK, WIDE)

    for s in range(8):

        @pl.when(jnp.logical_not(jnp.logical_and(mine, slot == s)))
        def _():
            come(zin.at[s], zs.at[0], zr.at[s])

        zflat[MINI * s : MINI * (s + 1), :] = zin[s].astype(F32)
    own = x * 2 + c
    xb[own] = zflat[...].astype(BF16)

    def tokens_in(v, core, g):
        first, size = GROUPS[g]
        return xb.at[v * 2 + core, pl.ds(first, size)]

    for g in range(2):
        for d in range(3):
            go(tokens_in(x, c, g), tokens_in(x, c, g), xs.at[d, g], xr.at[x, g], xdev[d])
        go(tokens_in(x, c, g), tokens_in(x, c, g), cs.at[x, g], cr.at[x, g], partner)

    @pl.when(zh == 0)
    def _():
        pl.semaphore_wait(answer, len(far))

    for i, device in enumerate(far):
        go(sq.at[mp], sq.at[mp], qs.at[3 + i], qr.at[mp], device)

    def cotangent(g, which):
        first, size = HALVES[g]
        return cots.at[which, pl.ds(first, size)]

    go(cotangent(0, zh), cotangent(0, zh), ts.at[0], tr.at[0], across)

    def tokens_ready(g):
        for v in [lax.rem(x + 3, NX), xnext[0], xnext[1]]:
            come(tokens_in(v, c, g), xs.at[0, g], xr.at[v, g])
            go(tokens_in(v, c, g), tokens_in(v, c, g), cs.at[v, g], cr.at[v, g], partner)
        for v in range(NX):
            come(tokens_in(v, 1 - c, g), cs.at[0, g], cr.at[v, g])

    def place(q):
        first, size = PIECES[q // NH]
        return first, size, q % NH

    def rows_of(q):
        first, size, h = place(q)
        return xb[NY * h : NY * (h + 1), first : first + size, :].reshape(NY * size, WIDE)

    def products(q):
        first, size, h = place(q)
        rows = pl.ds(first, size)
        lhs = rows_of(q)
        low = dot(lhs, down_both, NT).astype(BF16)
        low_t[q, :, 0 : NY * size] = dot(down_both, lhs, NT).astype(BF16)
        for k in range(2):
            value = dot(lhs, w[k]) + dot(low, up_wide[k])
            part[h, :, k, rows] = value.astype(BF16).reshape(NY, size, WIDE)
        for d in range(3):
            go(
                part.at[h, ynext[d], :, rows], ypart.at[h, d, :, rows],
                ps.at[q, d], pr.at[q, d], ydev[d],
            )

    def over_y(q):
        first, size, h = place(q)
        rows = pl.ds(first, size)
        total = part[h, y, :, rows].astype(F32)
        for d in range(3):
            come(ypart.at[h, d, :, rows], ps.at[q, d], pr.at[q, d])
            total = total + ypart[h, d, :, rows].astype(F32)
        zpart_out[h, :, rows] = total.astype(BF16)
        go(zpart_out.at[h, :, rows], zpart_in.at[h, :, rows], ss.at[q], sr.at[q], across)

    def activate(q, norm, ratio):
        first, size, h = place(q)
        rows = pl.ds(first, size)
        come(zpart_in.at[h, :, rows], ss.at[q], sr.at[q])
        if q == 2 * NH:
            come(cotangent(1, 1 - zh), ts.at[1], tr.at[1])
        pre = [
            zpart_out[h, k, rows].astype(F32) + zpart_in[h, k, rows].astype(F32)
            for k in range(2)
        ]
        gate = pre[0] * ratio[0:1]
        lift = pre[1] * ratio[1:2]
        active, slope = gelu_pair(gate)

        @pl.when(zh == h)
        def _():
            hid[rows, :] = (active * lift).astype(BF16)

        g = cots[h, rows, :].astype(F32)
        outs = [g * lift * slope, g * active]
        for k in range(2):
            mom[k : k + 1, :] += jnp.sum(outs[k] * pre[k], axis=0, keepdims=True)
            grad[h, y, k, rows] = (outs[k] * ratio[k : k + 1]).astype(BF16)
        for d in range(3):
            go(
                grad.at[h, y, :, rows], grad.at[h, y, :, rows],
                gs.at[q, d], gr.at[q, y], ydev[d],
            )

    def backward(q):
        first, size, h = place(q)
        rows = pl.ds(first, size)
        for d in range(3):
            come(grad.at[h, ynext[d], :, rows], gs.at[q, d], gr.at[q, ynext[d]])
        lhs = rows_of(q)
        total = None
        for k in range(2):
            g = grad[h, :, k, rows].reshape(NY * size, WIDE)
            low = dot(g, up[k], NT).astype(BF16)
            low_rows = dot(up[k], g, NT).astype(BF16)
            value = dot(g, w[k], NT) + SCALE * dot(low, down[k])
            total = value if total is None else total + value
            acc_d[k] += dot(low_rows, lhs)
            acc_u[k] += dot(low_t[q, RANK * k : RANK * (k + 1), 0 : NY * size], g)
        tb[h, :, :, rows] = total.astype(BF16).reshape(2, 2, size, WIDE)
        go(tb.at[h, :, 1 - c, rows], tpair.at[h, :, rows], fs.at[q], fr.at[q], partner)

    along_x = []

    def over_cores(q):
        first, size, h = place(q)
        rows = pl.ds(first, size)
        come(tpair.at[h, :, rows], fs.at[q], fr.at[q])
        for j in range(2):
            tsum[h, j, rows] = (
                tb[h, j, c, rows].astype(F32) + tpair[h, j, rows].astype(F32)
            ).astype(BF16)
            target = NH * h + j
            copy = send(
                tsum.at[h, j, rows], tx.at[x, rows],
                fxs.at[q, j], fxr.at[q // NH, x], at(x=target),
            )
            along_x.append((target, copy))

            @pl.when(x != target)
            def _():
                copy.start()

    along_z = []

    def to_owner(p):
        first, size = PIECES[p]
        rows = pl.ds(first, size)
        total = tsum[x // 2, lax.rem(x, 2), rows].astype(F32)
        for v in xnext:
            come(tx.at[v, rows], fxs.at[0, 0], fxr.at[p, v])
            total = total + tx[v, rows].astype(F32)
        tflat[rows, :] = total
        for s in LEAVES[p]:
            zout[s] = tflat[MINI * s : MINI * (s + 1), :].astype(BF16)
            copy = send(
                zout.at[s], zback.at[zl], bs.at[s], br.at[zl], at(zl=4 * c + s // 2, c=s % 2)
            )
            along_z.append((s, copy))

            @pl.when(jnp.logical_not(jnp.logical_and(mine, slot == s)))
            def _():
                copy.start()

    tokens_ready(0)
    norm = ratio = None
    for item in ORDER:
        q = int(item[1:]) if len(item) > 1 else None
        if item == "G":
            tokens_ready(1)
        elif item == "N":
            for device in range(NH * NY):

                @pl.when(device != mp)
                def _():
                    come(sq.at[device], qs.at[0], qr.at[device])

            norm_square = sq[0]
            for device in range(1, NH * NY):
                norm_square = norm_square + sq[device]
            norm = jnp.sqrt(norm_square + EPSILON)
            ratio = mag[...] / norm
            come(cotangent(0, 1 - zh), ts.at[0], tr.at[0])
        elif item == "H":
            go(cotangent(1, zh), cotangent(1, zh), ts.at[1], tr.at[1], across)
        elif item == "M":
            mom_all[y] = mom[...]
            for d in range(3):
                go(mom_all.at[y], mom_all.at[y], ms.at[d], mr.at[y], ydev[d])
        elif item == "W":
            for v in ynext:
                come(mom_all.at[v], ms.at[0], mr.at[v])
            moment = mom_all[0]
            for v in range(1, NY):
                moment = moment + mom_all[v]
            mg[...] = moment / norm
            term = -mag[...] * moment / (norm * norm * norm)
            for k in range(2):
                acc_u[k] += cross[k] * term[k : k + 1]
                weighted = up[k].astype(F32) * term[k : k + 1]
                spread = wide_dot(weighted, w[k], NT)
                acc_d[k] += spread + SCALE * wide_dot(wide_dot(weighted, up[k], NT), down[k])
        elif item[0] == "P":
            products(q)
        elif item[0] == "S":
            over_y(q)
        elif item[0] == "C":
            activate(q, norm, ratio)
        elif item[0] == "B":
            backward(q)
        elif item[0] == "U":
            over_cores(q)
        else:
            to_owner(q)

    d_pair_out[...] = acc_d[1 - c].astype(BF16)
    go(d_pair_out, d_pair_in, ds1, dr1, partner)
    for k in range(2):
        u_out[2 * k : 2 * k + 2] = (SCALE * acc_u[k]).reshape(2, 8, WIDE)
    for d in range(3):
        go(u_out.at[ynext[d]], u_y.at[y], us1.at[d], ur1.at[y], ydev[d])
    u_y[y] = u_out[y]

    come(d_pair_in, ds1, dr1)
    total = SCALE * (acc_d[c] + d_pair_in[...].astype(F32))
    for i in range(NX):
        d_x_out[i] = total[4 * i : 4 * (i + 1)]
    for d in range(3):
        go(d_x_out.at[xnext[d]], d_x.at[x], ds2.at[d], dr2.at[x], xdev[d])
    d_x[x] = d_x_out[x]

    over_cores(CHUNKS - 1)

    for v in ynext:
        come(u_y.at[v], us1.at[0], ur1.at[v])
    total = u_y[0]
    for v in range(1, NY):
        total = total + u_y[v]
    u_z[zh] = total
    go(u_z.at[zh], u_z.at[zh], us2, ur2.at[zh], across)

    for v in xnext:
        come(d_x.at[v], ds2.at[0], dr2.at[v])
    total = d_x[0]
    for v in range(1, NX):
        total = total + d_x[v]
    d_z[zl] = total
    for k in range(1, NZ):
        go(d_z.at[zl], d_z.at[zl], ds3.at[k - 1], dr3.at[zl], at(zl=lax.rem(zl + k, NZ)))

    to_owner(len(PIECES) - 1)

    @pl.when(mine)
    def _():
        zback[zl] = zout[slot]

    for k in range(1, NZ):
        v = lax.rem(zl + k, NZ)
        come(d_z.at[v], ds3.at[0], dr3.at[v])
    total = d_z[0]
    for t in range(1, NZ):
        total = total + d_z[t]
    d_all[c, x] = total
    for i, device in enumerate([partner] + xdev + xpair):
        go(d_all.at[c, x], d_all.at[c, x], ds4.at[i], dr4.at[c, x], device)

    come(u_z.at[1 - zh], us2, ur2.at[1 - zh])
    u_all[y] = u_z[0] + u_z[1]
    for d in range(3):
        go(u_all.at[y], u_all.at[y], us3.at[d], ur3.at[y], ydev[d])

    for t in range(NZ):

        @pl.when(jnp.logical_not(jnp.logical_and(mine, zl == t)))
        def _():
            come(zback.at[t], bs.at[0], br.at[t])

    total = zback[0].astype(F32)
    for t in range(1, NZ):
        total = total + zback[t].astype(F32)
    tg[...] = total

    for v in ynext:
        come(u_all.at[v], us3.at[0], ur3.at[v])
    for k in range(2):
        ug[k] = u_all[2 * k : 2 * k + 2].reshape(RANK, WIDE)
    come(d_all.at[1 - c, x], ds4.at[0], dr4.at[1 - c, x])
    for v in xnext:
        for core in range(2):
            come(d_all.at[core, v], ds4.at[0], dr4.at[core, v])
    for k in range(2):
        for i in range(NX):
            dg[k, 4 * i : 4 * (i + 1), :] = d_all[k, i]

    for t in range(NZ):

        @pl.when(jnp.logical_not(jnp.logical_and(mine, zl == t)))
        def _():
            zcopies[t].wait_send()

    for s, copy in along_z:

        @pl.when(jnp.logical_not(jnp.logical_and(mine, slot == s)))
        def _():
            copy.wait_send()

    for target, copy in along_x:

        @pl.when(x != target)
        def _():
            copy.wait_send()

    for copy in sent:
        copy.wait_send()


def keep(*refs):
    for source, target in zip(refs[:5], refs[5:]):
        target[...] = source[...]


def on_device(tokens, frozen_weight, adapter_down, adapter_up, magnitude, hidden_gradient):
    vmem = pl.BlockSpec(memory_space=pltpu.VMEM)
    dma = pltpu.SemaphoreType.DMA
    scratch = [
        pltpu.VMEM((MINI, WIDE), BF16),
        pltpu.VMEM((2, WIDE, WIDE), BF16),
        pltpu.VMEM((2, RANK, WIDE), BF16),
        pltpu.VMEM((2, RANK, WIDE), BF16),
        pltpu.VMEM((2, WIDE), F32),
        pltpu.VMEM((8, MINI, WIDE), BF16),
        pltpu.VMEM((ROWS, WIDE), F32),
        pltpu.VMEM((8, ROWS, WIDE), BF16),
        pltpu.VMEM((8, 2, WIDE), F32),
        pltpu.VMEM((CHUNKS, 2 * RANK, 128), BF16),
        pltpu.VMEM((2, 2 * RANK, WIDE), BF16),
        pltpu.VMEM((NH, NY, 2, ROWS, WIDE), BF16),
        pltpu.VMEM((NH, 3, 2, ROWS, WIDE), BF16),
        pltpu.VMEM((NH, 2, ROWS, WIDE), BF16),
        pltpu.VMEM((NH, 2, ROWS, WIDE), BF16),
        pltpu.VMEM((NH, ROWS, WIDE), BF16),
        pltpu.VMEM((NH, NY, 2, ROWS, WIDE), BF16),
        pltpu.VMEM((2, WIDE), F32),
        pltpu.VMEM((NY, 2, WIDE), F32),
        pltpu.VMEM((2, RANK, WIDE), F32),
        pltpu.VMEM((2, RANK, WIDE), F32),
        pltpu.VMEM((2, RANK, WIDE), F32),
        pltpu.VMEM((NH, 2, 2, ROWS, WIDE), BF16),
        pltpu.VMEM((NH, 2, ROWS, WIDE), BF16),
        pltpu.VMEM((NH, 2, ROWS, WIDE), BF16),
        pltpu.VMEM((NX, ROWS, WIDE), BF16),
        pltpu.VMEM((ROWS, WIDE), F32),
        pltpu.VMEM((8, MINI, WIDE), BF16),
        pltpu.VMEM((NZ, MINI, WIDE), BF16),
        pltpu.VMEM((RANK, WIDE), BF16),
        pltpu.VMEM((RANK, WIDE), BF16),
        pltpu.VMEM((NX, 4, WIDE), F32),
        pltpu.VMEM((NX, 4, WIDE), F32),
        pltpu.VMEM((NZ, 4, WIDE), F32),
        pltpu.VMEM((2, NX, 4, WIDE), F32),
        pltpu.VMEM((NY, 8, WIDE), F32),
        pltpu.VMEM((NY, 8, WIDE), F32),
        pltpu.VMEM((NH, 8, WIDE), F32),
        pltpu.VMEM((NY, 8, WIDE), F32),
        dma((6,)),
        dma((NZ,)), dma((8,)),
        dma((3, 2)), dma((NX, 2)),
        dma((NX, 2)), dma((NX, 2)),
        dma((7,)), dma((8,)),
        dma((2,)), dma((2,)),
        pltpu.SemaphoreType.REGULAR,
        dma((CHUNKS, 3)), dma((CHUNKS, 3)),
        dma((CHUNKS,)), dma((CHUNKS,)),
        dma((CHUNKS, 3)), dma((CHUNKS, NY)),
        dma((3,)), dma((NY,)),
        dma((CHUNKS,)), dma((CHUNKS,)),
        dma((CHUNKS, 2)), dma((len(PIECES), NX)),
        dma((8,)), dma((NZ,)),
        dma, dma,
        dma((3,)), dma((NX,)),
        dma((NZ - 1,)), dma((NZ,)),
        dma((7,)), dma((2, NX)),
        dma((3,)), dma((NY,)),
        dma, dma((NH,)),
        dma((3,)), dma((NY,)),
    ]
    shapes = (
        jax.ShapeDtypeStruct((ROWS, WIDE), BF16),
        jax.ShapeDtypeStruct((MINI, WIDE), F32),
        jax.ShapeDtypeStruct((2, RANK, WIDE), F32),
        jax.ShapeDtypeStruct((2, RANK, WIDE), F32),
        jax.ShapeDtypeStruct((2, WIDE), F32),
    )
    results = pl.pallas_call(
        kernel,
        name="dora_step",
        out_shape=shapes,
        in_specs=[pl.BlockSpec(memory_space=pl.ANY)] * 6,
        out_specs=(vmem,) * 5,
        scratch_shapes=scratch,
        compiler_params=pltpu.CompilerParams(
            collective_id=0, has_side_effects=True, vmem_limit_bytes=60 * 1024 * 1024
        ),
    )(tokens, frozen_weight, adapter_down, adapter_up, magnitude, hidden_gradient)
    return pl.pallas_call(
        keep, name="keep", out_shape=shapes, in_specs=[vmem] * 5, out_specs=(vmem,) * 5
    )(*results)


def solution(mesh):
    in_specs = (
        P("dp", "mp"),
        P(None, "mp", "dp"),
        P(None, None, "mp"),
        P(None, None, "dp"),
        P(None, "dp"),
        P("mp", "dp"),
    )
    out_specs = (
        P("mp", "dp"),
        P("dp", "mp"),
        P(None, None, "mp"),
        P(None, None, "dp"),
        P(None, "dp"),
    )
    return jax.shard_map(
        on_device, mesh=mesh, in_specs=in_specs, out_specs=out_specs, check_vma=False
    )
```

time: 147 us -> 128 us (0.87); the launches traced: 144 us -> 128 us
  Pallas kernels: 136 us -> 127 us
  local copies, waits for them, and re-layouts: 7.29 us -> 0 us
    pallas_call x1 -> x2, Pallas kernels: 136 us -> 127 us  [the longest x1 125 us: on_device(): pl.pallas_call(kernel, name='dora_step', out_shape=shapes, in_specs=[pl.B...]
    unnamed x5 -> x0, local copies, waits for them, and re-layouts: 7.29 us -> none
where the time goes in v2:
time: 128 us
  Pallas kernels  127 us (99%)
    pallas_call x1, Pallas kernels, on_device(): pl.pallas_call(kernel, name='dora_step', out_shape=shapes, in_specs=[pl.B...  125 us

profile of v2, /device:TPU:1, one launch (start us, length us, event | category | flops | bytes accessed | tf_op | source)
XLA Modules:
  0.0 127.8 jit_solution(17052660845460852025)
XLA Ops:
  0.6 125.4 %dora_step.1 = (bf16[96,576]{1,0:T(8,128)(2,1)}, f32[12,576]{1,0:T(8,128)}, f32[2,16,576]{2,1,0:T(8,128)}, f32[2,16,576]{2,1,0:T(8,128)}, f32[2,576]{1,0:T(2,128)}) custom-call(bf16[12,576]{1,0:T(8,128)(2,1)} %tok_in.1, bf16[2,576,576]{2,1,0:T(8,128)(2,1)} %w_in.1, bf16[2,16,576]{2,1,0:T(8,128)(2,1)} %down_in.1, bf16[2,16,576]{2,1,0:T(8,128)(2,1)} %up_in.1, ...), custom_call_target="tpu_custom_call" | custom-call | tf_op jit(solution)/shard_map/dora_step/pallas_call | solution.py:563
  126.1 1.7 %keep.1 = (bf16[96,576]{1,0:T(8,128)(2,1)}, f32[12,576]{1,0:T(8,128)}, f32[2,16,576]{2,1,0:T(8,128)}, f32[2,16,576]{2,1,0:T(8,128)}, f32[2,576]{1,0:T(2,128)}) custom-call(bf16[96,576]{1,0:T(8,128)(2,1)} %get-tuple-element.10.refs_0_, f32[12,576]{1,0:T(8,128)} %get-tuple-element.11.refs_1_, f32[2,16,576]{2,1,0:T(8,128)} %get-tuple-element.12.refs_2_, ...), custom_call_target="tpu_custom_call" | custom-call | tf_op jit(solution)/shard_map/keep/pallas_call | solution.py:574

commit v3 on v2

--- a/solution.py
+++ b/solution.py
@@ -19,15 +19,17 @@
 MINI = 12
 WIDE = 576
 RANK = 16
-PIECES = ((0, 16), (16, 32), (48, 32), (80, 16))
-LEAVES = ((0,), (1, 2, 3), (4, 5), (6, 7))
+PIECES = ((0, 16), (16, 16), (32, 16), (48, 16), (64, 16), (80, 16))
+LEAVES = ((0,), (1,), (2, 3), (4,), (5,), (6, 7))
 CHUNKS = len(PIECES) * NH
 GROUPS = ((0, 16), (16, 80))
-HALVES = ((0, 48), (48, 48))
+FAR_FIRST = (7, 0, 6, 1, 5, 2, 4, 3)
 ORDER = (
-    "P0 P1 G P2 S0 P3 S1 P4 S2 P5 S3 H P6 S4 P7 S5 N C0 C1 S6 S7 B0 C2 B1 U0 C3 B2 U1 C4 B3 U2 V0 "
-    "C5 B4 U3 C6 B5 U4 V1 C7 M B6 U5 W U6 B7 V2"
+    "P0 G P2 P4 S0 P6 S2 P8 P10 P1 S4 P3 S6 P5 S8 P7 S10 P9 P11 S1 N C0 S3 C1 S5 C2 S7 C3 S9 C4 "
+    "S11 C5 B1 B3 U1 E0 B5 U3 E1 B7 U5 E2 B9 U7 B0 E3 B11 U9 B2 U11 U0 E4 B4 U2 W E5 B6 V0 U4 B8 V1 "
+    "U6 B10"
 ).split()
+LAG = 2
 
 
 def dot(a, b, dims=NN):
@@ -57,12 +59,12 @@
 def kernel(
     tok_in, w_in, down_in, up_in, mag_in, cot_in,
     hid, tg, dg, ug, mg,
-    tok, w, down, up, mag,
-    zin, zflat, xb, sq, low_t, up_wide, part, ypart, zpart_out, zpart_in, cots, grad,
+    tok, w, down, up, mag, cot,
+    zin, zflat, xb, sq, low_t, up_wide, part, ypart, zpart_out, zpart_in, zown, grad,
     mom, mom_all, acc_d, acc_u, cross, tb, tpair, tsum, tx, tflat, zout, zback,
-    d_pair_out, d_pair_in, d_x_out, d_x, d_z, d_all, u_out, u_y, u_z, u_all,
-    ls, zs, zr, xs, xr, cs, cr, qs, qr, ts, tr, answer, ps, pr, ss, sr, gs, gr, ms, mr,
-    fs, fr, fxs, fxr, bs, br, ds1, dr1, ds2, dr2, ds3, dr3, ds4, dr4, us1, ur1, us2, ur2, us3, ur3,
+    d_x_out, d_x, d_z, d_all, u_out, u_y, u_z, u_all,
+    ls, zs, zr, xs, xr, cs, cr, qs, qr, answer, ps, pr, ss, sr, gs, gr, gz, ms, mr,
+    fs, fr, fxs, fxr, bs, br, ds2, dr2, ds3, dr3, ds4, dr4, us1, ur1, us2, ur2, us3, ur3,
 ):
     dp = lax.axis_index("dp")
     mp = lax.axis_index("mp")
@@ -123,7 +125,7 @@
         pltpu.make_async_copy(a, b, ls.at[i])
         for i, (a, b) in enumerate(
             ((down_in, down), (up_in, up), (w_in, w), (tok_in, tok), (mag_in, mag),
-             (cot_in, cots.at[zh]))
+             (cot_in, cot))
         )
     ]
     for copy in local:
@@ -146,12 +148,13 @@
             pl.semaphore_signal(answer, 1, device_id=device, device_id_type=MESH)
 
     zcopies = []
-    for t in range(NZ):
-        zcopies.append(send(tok, zin.at[slot], zs.at[t], zr.at[slot], at(zl=t, c=half)))
+    for t in FAR_FIRST:
+        copy = send(tok, zin.at[slot], zs.at[t], zr.at[slot], at(zl=t, c=half))
+        zcopies.append((t, copy))
 
         @pl.when(jnp.logical_not(jnp.logical_and(mine, zl == t)))
         def _():
-            zcopies[t].start()
+            copy.start()
 
     @pl.when(mine)
     def _():
@@ -196,12 +199,6 @@
     for i, device in enumerate(far):
         go(sq.at[mp], sq.at[mp], qs.at[3 + i], qr.at[mp], device)
 
-    def cotangent(g, which):
-        first, size = HALVES[g]
-        return cots.at[which, pl.ds(first, size)]
-
-    go(cotangent(0, zh), cotangent(0, zh), ts.at[0], tr.at[0], across)
-
     def tokens_ready(g):
         for v in [lax.rem(x + 3, NX), xnext[0], xnext[1]]:
             come(tokens_in(v, c, g), xs.at[0, g], xr.at[v, g])
@@ -210,15 +207,15 @@
             come(tokens_in(v, 1 - c, g), cs.at[0, g], cr.at[v, g])
 
     def place(q):
-        first, size = PIECES[q // NH]
-        return first, size, q % NH
+        return (q // 2, q % 2) + PIECES[q // 2]
 
     def rows_of(q):
-        first, size, h = place(q)
-        return xb[NY * h : NY * (h + 1), first : first + size, :].reshape(NY * size, WIDE)
+        _, own_half, first, size = place(q)
+        h = zh if own_half else 1 - zh
+        return xb[pl.ds(NY * h, NY), first : first + size, :].reshape(NY * size, WIDE)
 
     def products(q):
-        first, size, h = place(q)
+        _, h, first, size = place(q)
         rows = pl.ds(first, size)
         lhs = rows_of(q)
         low = dot(lhs, down_both, NT).astype(BF16)
@@ -233,46 +230,56 @@
             )
 
     def over_y(q):
-        first, size, h = place(q)
+        p, h, first, size = place(q)
         rows = pl.ds(first, size)
         total = part[h, y, :, rows].astype(F32)
         for d in range(3):
             come(ypart.at[h, d, :, rows], ps.at[q, d], pr.at[q, d])
             total = total + ypart[h, d, :, rows].astype(F32)
-        zpart_out[h, :, rows] = total.astype(BF16)
-        go(zpart_out.at[h, :, rows], zpart_in.at[h, :, rows], ss.at[q], sr.at[q], across)
-
-    def activate(q, norm, ratio):
-        first, size, h = place(q)
+        if h:
+            zown[:, rows] = total
+        else:
+            zpart_out[:, rows] = total.astype(BF16)
+            go(zpart_out.at[:, rows], zpart_in.at[:, rows], ss.at[p], sr.at[p], across)
+
+    def activate(p, norm, ratio):
+        first, size = PIECES[p]
         rows = pl.ds(first, size)
-        come(zpart_in.at[h, :, rows], ss.at[q], sr.at[q])
-        if q == 2 * NH:
-            come(cotangent(1, 1 - zh), ts.at[1], tr.at[1])
-        pre = [
-            zpart_out[h, k, rows].astype(F32) + zpart_in[h, k, rows].astype(F32)
-            for k in range(2)
-        ]
+        come(zpart_in.at[:, rows], ss.at[p], sr.at[p])
+        pre = [zown[k, rows] + zpart_in[k, rows].astype(F32) for k in range(2)]
         gate = pre[0] * ratio[0:1]
         lift = pre[1] * ratio[1:2]
         active, slope = gelu_pair(gate)
-
-        @pl.when(zh == h)
-        def _():
-            hid[rows, :] = (active * lift).astype(BF16)
-
-        g = cots[h, rows, :].astype(F32)
+        hid[rows, :] = (active * lift).astype(BF16)
+        g = cot[rows, :].astype(F32)
         outs = [g * lift * slope, g * active]
         for k in range(2):
             mom[k : k + 1, :] += jnp.sum(outs[k] * pre[k], axis=0, keepdims=True)
-            grad[h, y, k, rows] = (outs[k] * ratio[k : k + 1]).astype(BF16)
+            grad[1, y, k, rows] = (outs[k] * ratio[k : k + 1]).astype(BF16)
+        block = grad.at[1, y, :, rows]
         for d in range(3):
-            go(
-                grad.at[h, y, :, rows], grad.at[h, y, :, rows],
-                gs.at[q, d], gr.at[q, y], ydev[d],
-            )
+            go(block, block, gs.at[2 * p + 1, d], gr.at[2 * p + 1, y], ydev[d])
+        last = p == len(PIECES) - 1
+        if last:
+            mom_all[mp] = mom[...]
+            for i, device in enumerate(far + ydev):
+                go(mom_all.at[mp], mom_all.at[mp], ms.at[i], mr.at[mp], device)
+        for v in range(max(p - LAG, 0) if last else p - LAG, p + 1 if last else p - LAG + 1):
+            if v >= 0:
+                back = pl.ds(*PIECES[v])
+                go(
+                    grad.at[1, y, :, back], grad.at[0, y, :, back],
+                    gz.at[v], gr.at[2 * v, y], across,
+                )
+
+    def forward(p):
+        block = grad.at[0, y, :, pl.ds(*PIECES[p])]
+        come(block, gz.at[p], gr.at[2 * p, y])
+        for d in range(3):
+            go(block, block, gs.at[2 * p, d], gr.at[2 * p, y], ydev[d])
 
     def backward(q):
-        first, size, h = place(q)
+        _, h, first, size = place(q)
         rows = pl.ds(first, size)
         for d in range(3):
             come(grad.at[h, ynext[d], :, rows], gs.at[q, d], gr.at[q, ynext[d]])
@@ -292,17 +299,17 @@
     along_x = []
 
     def over_cores(q):
-        first, size, h = place(q)
+        p, h, first, size = place(q)
         rows = pl.ds(first, size)
         come(tpair.at[h, :, rows], fs.at[q], fr.at[q])
         for j in range(2):
             tsum[h, j, rows] = (
                 tb[h, j, c, rows].astype(F32) + tpair[h, j, rows].astype(F32)
             ).astype(BF16)
-            target = NH * h + j
+            target = NH * (zh if h else 1 - zh) + j
             copy = send(
                 tsum.at[h, j, rows], tx.at[x, rows],
-                fxs.at[q, j], fxr.at[q // NH, x], at(x=target),
+                fxs.at[q, j], fxr.at[p, x], at(x=target),
             )
             along_x.append((target, copy))
 
@@ -315,7 +322,7 @@
     def to_owner(p):
         first, size = PIECES[p]
         rows = pl.ds(first, size)
-        total = tsum[x // 2, lax.rem(x, 2), rows].astype(F32)
+        total = tsum[1 - lax.rem(x // 2 + zh, 2), lax.rem(x, 2), rows].astype(F32)
         for v in xnext:
             come(tx.at[v, rows], fxs.at[0, 0], fxr.at[p, v])
             total = total + tx[v, rows].astype(F32)
@@ -349,19 +356,16 @@
                 norm_square = norm_square + sq[device]
             norm = jnp.sqrt(norm_square + EPSILON)
             ratio = mag[...] / norm
-            come(cotangent(0, 1 - zh), ts.at[0], tr.at[0])
-        elif item == "H":
-            go(cotangent(1, zh), cotangent(1, zh), ts.at[1], tr.at[1], across)
-        elif item == "M":
-            mom_all[y] = mom[...]
-            for d in range(3):
-                go(mom_all.at[y], mom_all.at[y], ms.at[d], mr.at[y], ydev[d])
         elif item == "W":
-            for v in ynext:
-                come(mom_all.at[v], ms.at[0], mr.at[v])
+            for device in range(NH * NY):
+
+                @pl.when(device != mp)
+                def _():
+                    come(mom_all.at[device], ms.at[0], mr.at[device])
+
             moment = mom_all[0]
-            for v in range(1, NY):
-                moment = moment + mom_all[v]
+            for device in range(1, NH * NY):
+                moment = moment + mom_all[device]
             mg[...] = moment / norm
             term = -mag[...] * moment / (norm * norm * norm)
             for k in range(2):
@@ -375,6 +379,8 @@
             over_y(q)
         elif item[0] == "C":
             activate(q, norm, ratio)
+        elif item[0] == "E":
+            forward(q)
         elif item[0] == "B":
             backward(q)
         elif item[0] == "U":
@@ -382,23 +388,18 @@
         else:
             to_owner(q)
 
-    d_pair_out[...] = acc_d[1 - c].astype(BF16)
-    go(d_pair_out, d_pair_in, ds1, dr1, partner)
+    for k in range(2):
+        for i in range(NX):
+            d_x_out[k, i] = SCALE * acc_d[k, 4 * i : 4 * (i + 1), :]
+    d_x[c, x] = d_x_out[c, x]
+    others = [(1 - c, x)] + [(c, v) for v in xnext] + [(1 - c, v) for v in xnext]
+    for i, (core, v) in enumerate(others):
+        go(d_x_out.at[core, v], d_x.at[c, x], ds2.at[i], dr2.at[c, x], at(x=v, c=core))
     for k in range(2):
         u_out[2 * k : 2 * k + 2] = (SCALE * acc_u[k]).reshape(2, 8, WIDE)
     for d in range(3):
         go(u_out.at[ynext[d]], u_y.at[y], us1.at[d], ur1.at[y], ydev[d])
     u_y[y] = u_out[y]
-
-    come(d_pair_in, ds1, dr1)
-    total = SCALE * (acc_d[c] + d_pair_in[...].astype(F32))
-    for i in range(NX):
-        d_x_out[i] = total[4 * i : 4 * (i + 1)]
-    for d in range(3):
-        go(d_x_out.at[xnext[d]], d_x.at[x], ds2.at[d], dr2.at[x], xdev[d])
-    d_x[x] = d_x_out[x]
-
-    over_cores(CHUNKS - 1)
 
     for v in ynext:
         come(u_y.at[v], us1.at[0], ur1.at[v])
@@ -408,15 +409,26 @@
     u_z[zh] = total
     go(u_z.at[zh], u_z.at[zh], us2, ur2.at[zh], across)
 
-    for v in xnext:
-        come(d_x.at[v], ds2.at[0], dr2.at[v])
-    total = d_x[0]
-    for v in range(1, NX):
-        total = total + d_x[v]
+    over_cores(CHUNKS - 4)
+    over_cores(CHUNKS - 2)
+
+    for core, v in others:
+        come(d_x.at[core, v], ds2.at[0], dr2.at[core, v])
+    total = d_x[0, 0]
+    for i in range(1, NC * NX):
+        total = total + d_x[i // NX, i % NX]
     d_z[zl] = total
-    for k in range(1, NZ):
-        go(d_z.at[zl], d_z.at[zl], ds3.at[k - 1], dr3.at[zl], at(zl=lax.rem(zl + k, NZ)))
-
+    dcopies = []
+    for t in FAR_FIRST:
+        copy = send(d_z.at[zl], d_z.at[zl], ds3.at[t], dr3.at[zl], at(zl=t))
+        dcopies.append((t, copy))
+
+        @pl.when(zl != t)
+        def _():
+            copy.start()
+
+    for p in range(2, len(PIECES) - 1):
+        to_owner(p)
     to_owner(len(PIECES) - 1)
 
     @pl.when(mine)
@@ -461,11 +473,17 @@
         for i in range(NX):
             dg[k, 4 * i : 4 * (i + 1), :] = d_all[k, i]
 
-    for t in range(NZ):
+    for t, copy in zcopies:
 
         @pl.when(jnp.logical_not(jnp.logical_and(mine, zl == t)))
         def _():
-            zcopies[t].wait_send()
+            copy.wait_send()
+
+    for t, copy in dcopies:
+
+        @pl.when(zl != t)
+        def _():
+            copy.wait_send()
 
     for s, copy in along_z:
 
@@ -497,6 +515,7 @@
         pltpu.VMEM((2, RANK, WIDE), BF16),
         pltpu.VMEM((2, RANK, WIDE), BF16),
         pltpu.VMEM((2, WIDE), F32),
+        pltpu.VMEM((ROWS, WIDE), BF16),
         pltpu.VMEM((8, MINI, WIDE), BF16),
         pltpu.VMEM((ROWS, WIDE), F32),
         pltpu.VMEM((8, ROWS, WIDE), BF16),
@@ -505,12 +524,12 @@
         pltpu.VMEM((2, 2 * RANK, WIDE), BF16),
         pltpu.VMEM((NH, NY, 2, ROWS, WIDE), BF16),
         pltpu.VMEM((NH, 3, 2, ROWS, WIDE), BF16),
-        pltpu.VMEM((NH, 2, ROWS, WIDE), BF16),
-        pltpu.VMEM((NH, 2, ROWS, WIDE), BF16),
-        pltpu.VMEM((NH, ROWS, WIDE), BF16),
+        pltpu.VMEM((2, ROWS, WIDE), BF16),
+        pltpu.VMEM((2, ROWS, WIDE), BF16),
+        pltpu.VMEM((2, ROWS, WIDE), F32),
         pltpu.VMEM((NH, NY, 2, ROWS, WIDE), BF16),
         pltpu.VMEM((2, WIDE), F32),
-        pltpu.VMEM((NY, 2, WIDE), F32),
+        pltpu.VMEM((8, 2, WIDE), F32),
         pltpu.VMEM((2, RANK, WIDE), F32),
         pltpu.VMEM((2, RANK, WIDE), F32),
         pltpu.VMEM((2, RANK, WIDE), F32),
@@ -521,10 +540,8 @@
         pltpu.VMEM((ROWS, WIDE), F32),
         pltpu.VMEM((8, MINI, WIDE), BF16),
         pltpu.VMEM((NZ, MINI, WIDE), BF16),
-        pltpu.VMEM((RANK, WIDE), BF16),
-        pltpu.VMEM((RANK, WIDE), BF16),
-        pltpu.VMEM((NX, 4, WIDE), F32),
-        pltpu.VMEM((NX, 4, WIDE), F32),
+        pltpu.VMEM((2, NX, 4, WIDE), F32),
+        pltpu.VMEM((2, NX, 4, WIDE), F32),
         pltpu.VMEM((NZ, 4, WIDE), F32),
         pltpu.VMEM((2, NX, 4, WIDE), F32),
         pltpu.VMEM((NY, 8, WIDE), F32),
@@ -536,18 +553,16 @@
         dma((3, 2)), dma((NX, 2)),
         dma((NX, 2)), dma((NX, 2)),
         dma((7,)), dma((8,)),
-        dma((2,)), dma((2,)),
         pltpu.SemaphoreType.REGULAR,
         dma((CHUNKS, 3)), dma((CHUNKS, 3)),
-        dma((CHUNKS,)), dma((CHUNKS,)),
-        dma((CHUNKS, 3)), dma((CHUNKS, NY)),
-        dma((3,)), dma((NY,)),
+        dma((len(PIECES),)), dma((len(PIECES),)),
+        dma((CHUNKS, 3)), dma((CHUNKS, NY)), dma((len(PIECES),)),
+        dma((7,)), dma((8,)),
         dma((CHUNKS,)), dma((CHUNKS,)),
         dma((CHUNKS, 2)), dma((len(PIECES), NX)),
         dma((8,)), dma((NZ,)),
-        dma, dma,
-        dma((3,)), dma((NX,)),
-        dma((NZ - 1,)), dma((NZ,)),
+        dma((7,)), dma((2, NX)),
+        dma((NZ,)), dma((NZ,)),
         dma((7,)), dma((2, NX)),
         dma((3,)), dma((NY,)),
         dma, dma((NH,)),

time: 128 us -> 116 us (0.906)
  Pallas kernels: 127 us -> 115 us
    pallas_call x1, Pallas kernels: 125 us -> 113 us  [on_device(): pl.pallas_call(kernel, name='dora_step', out_shape=shapes, in_specs=[pl.B...]
where the time goes in v3:
time: 116 us
  Pallas kernels  115 us (99%)
    pallas_call x1, Pallas kernels, on_device(): pl.pallas_call(kernel, name='dora_step', out_shape=shapes, in_specs=[pl.B...  113 us

profile of v3, /device:TPU:1, one launch (start us, length us, event | category | flops | bytes accessed | tf_op | source)
XLA Modules:
  0.0 115.7 jit_solution(16090533359045292815)
XLA Ops:
  0.6 113.3 %dora_step.1 = (bf16[96,576]{1,0:T(8,128)(2,1)}, f32[12,576]{1,0:T(8,128)}, f32[2,16,576]{2,1,0:T(8,128)}, f32[2,16,576]{2,1,0:T(8,128)}, f32[2,576]{1,0:T(2,128)}) custom-call(bf16[12,576]{1,0:T(8,128)(2,1)} %tok_in.1, bf16[2,576,576]{2,1,0:T(8,128)(2,1)} %w_in.1, bf16[2,16,576]{2,1,0:T(8,128)(2,1)} %down_in.1, bf16[2,16,576]{2,1,0:T(8,128)(2,1)} %up_in.1, ...), custom_call_target="tpu_custom_call" | custom-call | tf_op jit(solution)/shard_map/dora_step/pallas_call | solution.py:578
  113.9 1.7 %keep.1 = (bf16[96,576]{1,0:T(8,128)(2,1)}, f32[12,576]{1,0:T(8,128)}, f32[2,16,576]{2,1,0:T(8,128)}, f32[2,16,576]{2,1,0:T(8,128)}, f32[2,576]{1,0:T(2,128)}) custom-call(bf16[96,576]{1,0:T(8,128)(2,1)} %get-tuple-element.10.refs_0_, f32[12,576]{1,0:T(8,128)} %get-tuple-element.11.refs_1_, f32[2,16,576]{2,1,0:T(8,128)} %get-tuple-element.12.refs_2_, ...), custom_call_target="tpu_custom_call" | custom-call | tf_op jit(solution)/shard_map/keep/pallas_call | solution.py:589

commit v4 on v3

--- a/solution.py
+++ b/solution.py
@@ -29,7 +29,7 @@
     "S11 C5 B1 B3 U1 E0 B5 U3 E1 B7 U5 E2 B9 U7 B0 E3 B11 U9 B2 U11 U0 E4 B4 U2 W E5 B6 V0 U4 B8 V1 "
     "U6 B10"
 ).split()
-LAG = 2
+CROSS = ((), (), (0,), (1, 2), (3, 4), (5,))
 
 
 def dot(a, b, dims=NN):
@@ -124,18 +124,13 @@
     local = [
         pltpu.make_async_copy(a, b, ls.at[i])
         for i, (a, b) in enumerate(
-            ((down_in, down), (up_in, up), (w_in, w), (tok_in, tok), (mag_in, mag),
+            ((tok_in, tok), (down_in, down), (up_in, up), (w_in, w), (mag_in, mag),
              (cot_in, cot))
         )
     ]
     for copy in local:
         copy.start()
-
-    for copy in local:
-        copy.wait()
-    for k in range(2):
-        merged = w[k].astype(F32) + SCALE * dot(down[k], up[k], TN)
-        sq[mp, pl.ds(k, 1), :] = jnp.sum(merged * merged, axis=0, keepdims=True)
+    local[0].wait()
 
     @pl.when(zh == 0)
     def _():
@@ -159,6 +154,12 @@
     @pl.when(mine)
     def _():
         zin[slot] = tok[...]
+
+    for copy in local[1:]:
+        copy.wait()
+    for k in range(2):
+        merged = w[k].astype(F32) + SCALE * dot(down[k], up[k], TN)
+        sq[mp, pl.ds(k, 1), :] = jnp.sum(merged * merged, axis=0, keepdims=True)
 
     for i, device in enumerate(ydev):
         go(sq.at[mp], sq.at[mp], qs.at[i], qr.at[mp], device)
@@ -173,21 +174,22 @@
     acc_u[...] = jnp.zeros_like(acc_u)
     down_both = down[...].reshape(2 * RANK, WIDE)
 
-    for s in range(8):
-
-        @pl.when(jnp.logical_not(jnp.logical_and(mine, slot == s)))
-        def _():
-            come(zin.at[s], zs.at[0], zr.at[s])
-
-        zflat[MINI * s : MINI * (s + 1), :] = zin[s].astype(F32)
-    own = x * 2 + c
-    xb[own] = zflat[...].astype(BF16)
-
     def tokens_in(v, core, g):
         first, size = GROUPS[g]
         return xb.at[v * 2 + core, pl.ds(first, size)]
 
+    own = x * 2 + c
     for g in range(2):
+        for s in range(2 * g, 2 + 6 * g):
+
+            @pl.when(jnp.logical_not(jnp.logical_and(mine, slot == s)))
+            def _():
+                come(zin.at[s], zs.at[0], zr.at[s])
+
+            zflat[MINI * s : MINI * (s + 1), :] = zin[s].astype(F32)
+        first, size = GROUPS[g]
+        rows = slice(first, first + size)
+        xb[own, rows, :] = zflat[rows, :].astype(BF16)
         for d in range(3):
             go(tokens_in(x, c, g), tokens_in(x, c, g), xs.at[d, g], xr.at[x, g], xdev[d])
         go(tokens_in(x, c, g), tokens_in(x, c, g), cs.at[x, g], cr.at[x, g], partner)
@@ -264,13 +266,12 @@
             mom_all[mp] = mom[...]
             for i, device in enumerate(far + ydev):
                 go(mom_all.at[mp], mom_all.at[mp], ms.at[i], mr.at[mp], device)
-        for v in range(max(p - LAG, 0) if last else p - LAG, p + 1 if last else p - LAG + 1):
-            if v >= 0:
-                back = pl.ds(*PIECES[v])
-                go(
-                    grad.at[1, y, :, back], grad.at[0, y, :, back],
-                    gz.at[v], gr.at[2 * v, y], across,
-                )
+        for v in CROSS[p]:
+            back = pl.ds(*PIECES[v])
+            go(
+                grad.at[1, y, :, back], grad.at[0, y, :, back],
+                gz.at[v], gr.at[2 * v, y], across,
+            )
 
     def forward(p):
         block = grad.at[0, y, :, pl.ds(*PIECES[p])]

time: 116 us -> 116 us (level)
  no operation moved by 1% of the time
where the time goes in v4:
time: 116 us
  Pallas kernels  115 us (99%)
    pallas_call x1, Pallas kernels, on_device(): pl.pallas_call(kernel, name='dora_step', out_shape=shapes, in_specs=[pl.B...  113 us

profile of v4, /device:TPU:1, one launch (start us, length us, event | category | flops | bytes accessed | tf_op | source)
XLA Modules:
  0.0 115.6 jit_solution(14784158005684508395)
XLA Ops:
  0.6 113.2 %dora_step.1 = (bf16[96,576]{1,0:T(8,128)(2,1)}, f32[12,576]{1,0:T(8,128)}, f32[2,16,576]{2,1,0:T(8,128)}, f32[2,16,576]{2,1,0:T(8,128)}, f32[2,576]{1,0:T(2,128)}) custom-call(bf16[12,576]{1,0:T(8,128)(2,1)} %tok_in.1, bf16[2,576,576]{2,1,0:T(8,128)(2,1)} %w_in.1, bf16[2,16,576]{2,1,0:T(8,128)(2,1)} %down_in.1, bf16[2,16,576]{2,1,0:T(8,128)(2,1)} %up_in.1, ...), custom_call_target="tpu_custom_call" | custom-call | tf_op jit(solution)/shard_map/dora_step/pallas_call | solution.py:579
  113.8 1.7 %keep.1 = (bf16[96,576]{1,0:T(8,128)(2,1)}, f32[12,576]{1,0:T(8,128)}, f32[2,16,576]{2,1,0:T(8,128)}, f32[2,16,576]{2,1,0:T(8,128)}, f32[2,576]{1,0:T(2,128)}) custom-call(bf16[96,576]{1,0:T(8,128)(2,1)} %get-tuple-element.10.refs_0_, f32[12,576]{1,0:T(8,128)} %get-tuple-element.11.refs_1_, f32[2,16,576]{2,1,0:T(8,128)} %get-tuple-element.12.refs_2_, ...), custom_call_target="tpu_custom_call" | custom-call | tf_op jit(solution)/shard_map/keep/pallas_call | solution.py:590
